TPU v7x, 8 devices: a whole 2x2x1 slice. The times are simulated.
8 devices in a mesh: rep: 2 (over y, z), dp: 4 (over x, core).
Axes of the slice: x: 2, y: 2, z: 1, core: 2. Of those that a mesh axis runs over, the one named last changes fastest.
Arguments:
- x: bfloat16 [8, 2048, 512], P(('rep', 'dp')), parts along dimension 0
- dy: bfloat16 [8, 2048, 512], P(('rep', 'dp')), parts along dimension 0
- w_gate: bfloat16 [2, 512, 4096], P(None, 'dp')
- w_up: bfloat16 [2, 512, 4096], P(None, 'dp')
- w_down: bfloat16 [2, 4096, 512], P(None, 'dp')
- m_w_gate: float32 [2, 512, 4096], P(None, 'dp')
- m_w_up: float32 [2, 512, 4096], P(None, 'dp')
- m_w_down: float32 [2, 4096, 512], P(None, 'dp')
- v_w_gate: float32 [2, 512, 4096], P(None, 'dp')
- v_w_up: float32 [2, 512, 4096], P(None, 'dp')
- v_w_down: float32 [2, 4096, 512], P(None, 'dp')
Outputs:
- output 1: bfloat16 [4, 512, 4096], P('rep', 'dp'), parts along dimension 0
- output 2: bfloat16 [4, 512, 4096], P('rep', 'dp'), parts along dimension 0
- output 3: bfloat16 [4, 4096, 512], P('rep', 'dp'), parts along dimension 0
- output 4: float32 [4, 512, 4096], P('rep', 'dp'), parts along dimension 0
- output 5: float32 [4, 512, 4096], P('rep', 'dp'), parts along dimension 0
- output 6: float32 [4, 4096, 512], P('rep', 'dp'), parts along dimension 0
- output 7: float32 [4, 512, 4096], P('rep', 'dp'), parts along dimension 0
- output 8: float32 [4, 512, 4096], P('rep', 'dp'), parts along dimension 0
- output 9: float32 [4, 4096, 512], P('rep', 'dp'), parts along dimension 0
There are 2 independent parts. A program takes and returns all parts, laid end to end along the dimension named above; an argument that names none is the same for every part.
All inputs are finite; a program needn't handle non-finite values.
Results may differ from a plain program's by a relative error of at most 0.022.
Values are sent between devices in bfloat16 or wider.
A program may use at most 2 GiB of HBM per device.

v0:
```python
import jax
import jax.numpy as jnp
from jax import lax
from jax.sharding import PartitionSpec as P

NAMES = ("w_gate", "w_up", "w_down")


def matmul(a, w):
    return jnp.dot(a, w, preferred_element_type=jnp.float32).astype(jnp.bfloat16)


def normed(h):
    wide = h.astype(jnp.float32)
    scale = lax.rsqrt(jnp.mean(wide**2, -1, keepdims=True) + 1e-6)
    return (wide * scale).astype(jnp.bfloat16)


def layer(h, w):
    a = normed(h)
    gate = jnp.dot(a, w["w_gate"], preferred_element_type=jnp.float32)
    up = jnp.dot(a, w["w_up"], preferred_element_type=jnp.float32)
    return h + matmul((jax.nn.silu(gate) * up).astype(jnp.bfloat16), w["w_down"])


def adamw(w, m, v, g):
    m = 0.9 * m + 0.1 * g
    v = 0.95 * v + 0.05 * g * g
    step = m * lax.rsqrt(v + 1e-8) + 0.1 * w
    return (w - 0.02 * step).astype(jnp.bfloat16), m, v


def clipped(gradients, sum_of_squares, count):
    factor = jnp.minimum(1.0, 0.5 * lax.rsqrt(sum_of_squares / count + 1e-30))
    return [g * factor for g in gradients]


def solution(mesh):
    def fetched(weights, number):
        return {name: lax.all_gather(w[number], "dp", axis=0, tiled=True) for name, w in zip(NAMES, weights, strict=True)}

    def step(x, dy, *arrays):
        weights, m, v = (arrays[i : i + 3] for i in (0, 3, 6))
        layers = weights[0].shape[0]
        h, kept = x[0], []
        for number in range(layers):
            kept.append(h)
            h = layer(h, fetched(weights, number))
        by_h, mine = dy[0], [None] * layers
        for number in reversed(range(layers)):
            _, back = jax.vjp(lambda w, h: layer(h, w), fetched(weights, number), kept[number])
            by_w, by_h = back(by_h)
            mine[number] = [lax.psum_scatter(by_w[name], "dp", scatter_dimension=0, tiled=True) for name in NAMES]
        gradients = [jnp.stack([mine[number][i] for number in range(layers)]).astype(jnp.float32) for i in range(3)]
        squares = lax.psum(sum(jnp.sum(g * g) for g in gradients), "dp")
        gradients = clipped(gradients, squares, lax.psum(1, "dp") * sum(g.size for g in gradients))
        new = [adamw(w.astype(jnp.float32), m, v, g) for w, m, v, g in zip(weights, m, v, gradients, strict=True)]
        return tuple(one[which] for which in range(3) for one in new)

    states, cut = P(("rep", "dp"), None, None), P(None, "dp", None)
    return jax.shard_map(
        step,
        mesh=mesh,
        in_specs=(states, states) + (cut,) * 9,
        out_specs=(P("rep", "dp", None),) * 9,
        check_vma=False,
    )
```

profile of v0, /device:TPU:0, one launch (start us, length us, event | category | flops | bytes accessed | tf_op | source)
XLA Modules:
  0.0 591.0 jit_solution(10438742044949102930)
XLA Ops:
  7.2 3.1 fusion.105
  10.3 0.0 all-gather.15.cloned.1.call-start
  10.4 3.2 fusion.104
  13.6 0.0 all-gather.17.cloned.1.call-start
  13.7 1.5 fusion.103
  15.2 0.5 all-gather.23.cloned.1.call-update
  15.8 0.5 all-gather.21.cloned.1.call-update
  16.4 0.5 all-gather.19.cloned.1.call-update
  16.9 2.9 copy.20
  19.9 0.5 fusion.31
  20.4 4.2 copy.21
  24.5 20.3 %all-gather.13.cloned.1.call-done = bf16[1,512,4096]{2,1,0:T(8,128)(2,1)} async-done(((bf16[1,128,4096]{2,1,0:T(8,128)(2,1)}), bf16[1,512,4096]{2,1,0:T(8,128)(2,1)}) %all-gather.13.cloned.1.call-update) | async-done | bytes 4194320 | tf_op jit(solution)/shard_map/all_gather | solution.py:40
  44.8 17.5 %fusion.63 = f32[2048,4096]{1,0:T(8,128)} fusion(bf16[1,512,4096]{2,1,0:T(8,128)(2,1)} %all-gather.13.cloned.1.call-done, bf16[1,2048,512]{1,2,0:T(8,128)(2,1)S(1)} %copy.20, f32[2048]{0:T(1024)S(1)} %add_rsqrt_fusion), kind=kOutput, calls=%fused_computation.95 | convolution fusion | flops 8593080320 | bytes 39854080 | tf_op jit(solution)/shard_map/dot_general | solution.py:21
  62.3 16.1 %all-gather.15.cloned.1.call-done = bf16[1,512,4096]{2,1,0:T(8,128)(2,1)} async-done(((bf16[1,128,4096]{2,1,0:T(8,128)(2,1)}), bf16[1,512,4096]{2,1,0:T(8,128)(2,1)}) %all-gather.15.cloned.1.call-update) | async-done | bytes 4194320 | tf_op jit(solution)/shard_map/all_gather | solution.py:40
  78.5 32.2 %multiply_convert_fusion.1 = (bf16[2048,4096]{1,0:T(8,128)(2,1)}, f32[2048,4096]{1,0:T(8,128)}) fusion(f32[2048,4096]{1,0:T(8,128)} %fusion.63, bf16[1,512,4096]{2,1,0:T(8,128)(2,1)} %all-gather.15.cloned.1.call-done, bf16[1,2048,512]{1,2,0:T(8,128)(2,1)S(1)} %copy.20, f32[2048]{0:T(1024)S(1)} %add_rsqrt_fusion), kind=kOutput, calls=%fused_computation.17 | convolution fusion | flops 8643411968 | bytes 90185728 | tf_op jit(solution)/shard_map/dot_general | solution.py:22
  110.6 1.5 all-gather.17.cloned.1.call-done
  112.1 14.9 %fusion.47 = (f32[2048]{0:T(1024)S(1)}, bf16[2048,512]{0,1:T(8,128)(2,1)}) fusion(bf16[2048,4096]{1,0:T(8,128)(2,1)} %get-tuple-element.24, bf16[1,4096,512]{2,1,0:T(8,128)(2,1)} %all-gather.17.cloned.1.call-done, bf16[1,2048,512]{1,2,0:T(8,128)(2,1)S(1)} %copy.20), kind=kOutput, calls=%fused_computation.79 | convolution fusion | flops 8595175424 | bytes 25174016 | tf_op jit(solution)/shard_map/dot_general | solution.py:10
  127.0 18.6 %all-gather.23.cloned.1.call-done = bf16[1,512,4096]{2,1,0:T(8,128)(2,1)} async-done(((bf16[1,128,4096]{2,1,0:T(8,128)(2,1)}), bf16[1,512,4096]{2,1,0:T(8,128)(2,1)}) %all-gather.23.cloned.1.call-update) | async-done | bytes 4194320 | tf_op jit(solution)/shard_map/all_gather | solution.py:40
  145.6 17.9 %fusion.50 = f32[2048,4096]{1,0:T(8,128)} fusion(bf16[1,512,4096]{2,1,0:T(8,128)(2,1)} %all-gather.23.cloned.1.call-done, bf16[2048,512]{0,1:T(8,128)(2,1)} %get-tuple-element.27, f32[2048]{0:T(1024)S(1)} %fusion.91), kind=kOutput, calls=%fused_computation.82 | convolution fusion | flops 8593080320 | bytes 39854080 | tf_op jit(solution)/shard_map/jvp()/dot_general | solution.py:22
  163.5 15.5 %all-gather.21.cloned.1.call-done = bf16[1,4096,512]{2,1,0:T(8,128)(2,1)} async-done(((bf16[1,1024,512]{2,1,0:T(8,128)(2,1)}), bf16[1,4096,512]{2,1,0:T(8,128)(2,1)}) %all-gather.21.cloned.1.call-update) | async-done | bytes 4194320 | tf_op jit(solution)/shard_map/all_gather | solution.py:40
  179.1 13.9 %convolution_convert_fusion.1 = bf16[2048,4096]{1,0:T(8,128)(2,1)} fusion(bf16[1,4096,512]{2,1,0:T(8,128)(2,1)} %all-gather.21.cloned.1.call-done, bf16[1,2048,512]{2,1,0:T(8,128)(2,1)S(1)} %copy-done.10), kind=kOutput, calls=%fused_computation.25 | convolution fusion | flops 8598323200 | bytes 23068672 | tf_op jit(solution)/shard_map/transpose(jvp())/dot_general | solution.py:10
  193.0 19.6 %all-gather.19.cloned.1.call-done = bf16[1,512,4096]{2,1,0:T(8,128)(2,1)} async-done(((bf16[1,128,4096]{2,1,0:T(8,128)(2,1)}), bf16[1,512,4096]{2,1,0:T(8,128)(2,1)}) %all-gather.19.cloned.1.call-update) | async-done | bytes 4194320 | tf_op jit(solution)/shard_map/all_gather | solution.py:40
  212.6 41.4 %fusion.2 = (bf16[2048,4096]{1,0:T(8,128)(2,1)}, f32[2048,4096]{1,0:T(8,128)}) fusion(f32[2048,4096]{1,0:T(8,128)} %fusion.50, bf16[2048,4096]{1,0:T(8,128)(2,1)} %convolution_convert_fusion.1, bf16[1,512,4096]{2,1,0:T(8,128)(2,1)} %all-gather.19.cloned.1.call-done, bf16[2048,512]{0,1:T(8,128)(2,1)} %get-tuple-element.27, f32[2048]{0:T(1024)S(1)} %fusion.91), kind=kOutput, calls=%fused_computation.8 | convolution fusion | flops 8693743616 | bytes 106962944 | tf_op jit(solution)/shard_map/jvp()/dot_general | solution.py:21
  254.0 21.0 %fusion.71 = bf16[2048,512]{0,1:T(8,128)(2,1)S(1)} fusion(bf16[1,512,4096]{2,1,0:T(8,128)(2,1)} %all-gather.23.cloned.1.call-done, bf16[2048,4096]{1,0:T(8,128)(2,1)} %convolution_convert_fusion.1, f32[2048,4096]{1,0:T(8,128)} %get-tuple-element.29), kind=kOutput, calls=%fused_computation.99 | convolution fusion | flops 8641314816 | bytes 56623104 | tf_op jit(solution)/shard_map/transpose(jvp())/dot_general | solution.py:22
  275.0 13.3 %fusion.49 = (f32[2048]{0:T(1024)S(1)}, bf16[2048,512]{0,1:T(8,128)(2,1)S(1)}) fusion(bf16[2048,512]{0,1:T(8,128)(2,1)S(1)} %copy-done.12, bf16[2048,512]{0,1:T(8,128)(2,1)S(1)} %fusion.71, bf16[2048,4096]{1,0:T(8,128)(2,1)} %get-tuple-element.28, bf16[1,512,4096]{2,1,0:T(8,128)(2,1)S(1)} %copy-done.21), kind=kOutput, calls=%fused_computation.81 | convolution fusion | flops 8595175424 | bytes 27271168 | tf_op jit(solution)/shard_map/transpose(jvp())/dot_general | solution.py:21
  288.3 1.4 fusion.80
  289.7 1.3 copy-done.14
  291.1 14.0 %convolution_convert_fusion.2 = bf16[4096,512]{1,0:T(8,128)(2,1)} fusion(bf16[2048,4096]{1,0:T(8,128)(2,1)} %get-tuple-element.24, bf16[2048,512]{0,1:T(8,128)(2,1)S(1)} %fusion.80), kind=kOutput, calls=%fused_computation.36 | convolution fusion | flops 8592031744 | bytes 23068672 | tf_op jit(solution)/shard_map/transpose(jvp())/dot_general | solution.py:10
  305.1 1.5 copy-done.11
  306.6 26.0 %fusion.20 = bf16[4096,512]{1,0:T(8,128)(2,1)} fusion(f32[2048,4096]{1,0:T(8,128)} %fusion.50, bf16[1,2048,512]{2,1,0:T(8,128)(2,1)S(1)} %copy-done.11, f32[2048,4096]{1,0:T(8,128)} %get-tuple-element.29), kind=kOutput, calls=%fused_computation.38 | convolution fusion | flops 8642363392 | bytes 73400320 | tf_op jit(solution)/shard_map/transpose(jvp())/dot_general | solution.py:10
  332.7 0.0 reduce-scatter.11.cloned.1.call-start
  332.7 15.2 %convolution_convert_fusion = bf16[2048,4096]{1,0:T(8,128)(2,1)} fusion(bf16[2048,512]{0,1:T(8,128)(2,1)} %copy-done.14, bf16[1,4096,512]{2,1,0:T(8,128)(2,1)} %all-gather.17.cloned.1.call-done), kind=kOutput, calls=%fused_computation.24 | convolution fusion | flops 8598323200 | bytes 23068672 | tf_op jit(solution)/shard_map/transpose(jvp())/dot_general | solution.py:10
  347.9 21.5 %fusion.19 = bf16[512,4096]{1,0:T(8,128)(2,1)} fusion(bf16[2048,4096]{1,0:T(8,128)(2,1)} %convolution_convert_fusion, f32[2048,4096]{1,0:T(8,128)} %fusion.63, bf16[1,2048,512]{1,2,0:T(8,128)(2,1)S(1)} %copy-done.5, f32[2048]{0:T(1024)S(1)} %copy-done.20), kind=kOutput, calls=%fused_computation.35 | convolution fusion | flops 8645509120 | bytes 56631296 | tf_op jit(solution)/shard_map/transpose(jvp())/dot_general | solution.py:22
  369.5 0.6 copy-done.18
  370.2 22.3 %fusion.15 = bf16[512,4096]{1,0:T(8,128)(2,1)} fusion(bf16[2048,4096]{1,0:T(8,128)(2,1)} %convolution_convert_fusion.1, bf16[2048,512]{0,1:T(8,128)(2,1)} %get-tuple-element.27, f32[2048]{0:T(1024)S(1)} %copy-done.18, f32[2048,4096]{1,0:T(8,128)} %get-tuple-element.29), kind=kOutput, calls=%fused_computation.33 | convolution fusion | flops 8645509120 | bytes 56631296 | tf_op jit(solution)/shard_map/transpose(jvp())/dot_general | solution.py:22
  392.6 32.4 %fusion.16 = bf16[512,4096]{1,0:T(8,128)(2,1)} fusion(f32[2048,4096]{1,0:T(8,128)} %fusion.63, f32[2048,4096]{1,0:T(8,128)} %get-tuple-element.25, bf16[2048,4096]{1,0:T(8,128)(2,1)} %convolution_convert_fusion, bf16[1,2048,512]{1,2,0:T(8,128)(2,1)S(1)} %copy-done.5, f32[2048]{0:T(1024)S(1)} %copy-done.20), kind=kOutput, calls=%fused_computation.34 | convolution fusion | flops 8687452160 | bytes 90185728 | tf_op jit(solution)/shard_map/transpose(jvp())/dot_general | solution.py:21
  425.0 0.0 reduce-scatter.9.cloned.1.call-start
  425.1 1.5 copy-done.13
  426.6 13.9 %convolution_convert_fusion.3 = bf16[512,4096]{1,0:T(8,128)(2,1)} fusion(bf16[2048,4096]{1,0:T(8,128)(2,1)} %get-tuple-element.28, bf16[2048,512]{0,1:T(8,128)(2,1)S(1)} %copy-done.13, f32[2048]{0:T(1024)S(1)} %copy-done.18), kind=kOutput, calls=%fused_computation.37 | convolution fusion | flops 8593080320 | bytes 23076864 | tf_op jit(solution)/shard_map/transpose(jvp())/dot_general | solution.py:21
  440.6 3.4 fusion.37
  444.0 23.4 %reduce-scatter.13.cloned.1.call-done = bf16[128,4096]{1,0:T(8,128)(2,1)} async-done(((bf16[512,4096]{1,0:T(8,128)(2,1)}), bf16[128,4096]{1,0:T(8,128)(2,1)}) %reduce-scatter.13.cloned.1.call-update) | async-done | bytes 1048592 | tf_op jit(solution)/shard_map/reduce_scatter | solution.py:53
  467.4 3.2 fusion.36
  470.7 38.2 %reduce-scatter.7.cloned.1.call-done = bf16[128,4096]{1,0:T(8,128)(2,1)} async-done(((bf16[512,4096]{1,0:T(8,128)(2,1)}), bf16[128,4096]{1,0:T(8,128)(2,1)}) %reduce-scatter.7.cloned.1.call-update) | async-done | bytes 1048592 | tf_op jit(solution)/shard_map/reduce_scatter | solution.py:53
  508.8 41.2 %reduce-scatter.9.cloned.1.call-done = bf16[128,4096]{1,0:T(8,128)(2,1)} async-done(((bf16[512,4096]{1,0:T(8,128)(2,1)}), bf16[128,4096]{1,0:T(8,128)(2,1)}) %reduce-scatter.9.cloned.1.call-update) | async-done | bytes 1048592 | tf_op jit(solution)/shard_map/reduce_scatter | solution.py:53
  550.0 3.2 fusion.35
  555.2 6.3 %psum.7 = f32[]{:T(128)} all-reduce(f32[]{:T(128)S(6)} %add.99), channel_id=1, replica_groups=mesh['rep'=2,'dp'=4] {'dp'}, use_global_device_ids=true, to_apply=%region_12.13 | all-reduce | flops 1 | bytes 8 | tf_op jit(solution)/shard_map/psum | solution.py:55
  562.2 8.1 %fusion.43 = (bf16[2,1024,512]{2,1,0:T(8,128)(2,1)}, f32[2,1024,512]{2,1,0:T(8,128)}, f32[2,1024,512]{2,1,0:T(8,128)}) fusion(bf16[2,1024,512]{2,1,0:T(8,128)(2,1)S(1)} %copy-done.1, f32[]{:T(128)S(6)} %min_shard_map.3, bf16[1,1024,512]{2,1,0:T(8,128)(2,1)} %bitcast.75, bf16[1,1024,512]{2,1,0:T(8,128)(2,1)S(1)} %bitcast.73, f32[2,1024,512]{2,1,0:T(8,128)} %param.21, ...), kind=kLoop, calls=%fused_computation.75 | loop fusion | flops 20971520 | bytes 23068676 | tf_op jit(solution)/shard_map/convert_element_type | solution.py:30
  570.3 13.4 %fusion.30 = (bf16[2,128,4096]{2,1,0:T(8,128)(2,1)}, f32[2,128,4096]{2,1,0:T(8,128)}, f32[2,128,4096]{2,1,0:T(8,128)}, bf16[2,128,4096]{2,1,0:T(8,128)(2,1)}, f3...) fusion(bf16[2,128,4096]{2,1,0:T(8,128)(2,1)S(1)} %copy-done.2, f32[]{:T(128)S(6)} %min_shard_map.3, ...), kind=kLoop, calls=%fused_computation.62 | loop fusion | flops 41943040 | bytes 46137348 | tf_op jit(solution)/shard_map/convert_element_type | solution.py:30
  (63 shorter events, 0.6 us)
Async XLA Ops:
  7.2 37.6 %all-gather.13.cloned.1.call-start = ((), (), s32[]{:S(2)}) async-start(), calls=%async_computation.12 | async-start | bytes 5242880 | tf_op jit(solution)/shard_map/all_gather | solution.py:40
  10.3 3.4 copy-start
  10.3 68.1 %all-gather.15.cloned.1.call-start = ((), (), s32[]{:S(2)}) async-start(), calls=%async_computation.13 | async-start | bytes 5242880 | tf_op jit(solution)/shard_map/all_gather | solution.py:40
  13.6 98.5 %all-gather.17.cloned.1.call-start = ((), (), s32[]{:S(2)}) async-start(), calls=%async_computation.14 | async-start | bytes 5242880 | tf_op jit(solution)/shard_map/all_gather | solution.py:40
  15.1 130.4 %all-gather.23.cloned.1.call-start = ((), (), s32[]{:S(2)}) async-start(), calls=%async_computation.17 | async-start | bytes 5242880 | tf_op jit(solution)/shard_map/all_gather | solution.py:40
  15.7 163.3 %all-gather.21.cloned.1.call-start = ((), (), s32[]{:S(2)}) async-start(), calls=%async_computation.16 | async-start | bytes 5242880 | tf_op jit(solution)/shard_map/all_gather | solution.py:40
  16.3 196.2 %all-gather.19.cloned.1.call-start = ((), (), s32[]{:S(2)}) async-start(), calls=%async_computation.15 | async-start | bytes 5242880 | tf_op jit(solution)/shard_map/all_gather | solution.py:40
  16.9 423.7 %reduce-scatter.15.cloned.1.call-start = ((), (), s32[]{:S(2)}) async-start(), calls=%async_computation.10 | async-start | bytes 5242880 | tf_op jit(solution)/shard_map/reduce_scatter | solution.py:53
  19.9 92.2 %copy-start.4 = (bf16[1,2048,512]{1,2,0:T(8,128)(2,1)}, bf16[1,2048,512]{1,2,0:T(8,128)(2,1)S(1)}, u32[]{:S(2)}) copy-start(bf16[1,2048,512]{1,2,0:T(8,128)(2,1)S(1)} %copy.20) | copy-start | bytes 6291460
  20.4 58.1 %copy-start.19 = (f32[2048]{0:T(1024)}, f32[2048]{0:T(1024)S(1)}, u32[]{:S(2)}) copy-start(f32[2048]{0:T(1024)S(1)} %add_rsqrt_fusion) | copy-start | bytes 24580
  127.0 36.6 %copy-start.15 = (f32[2048]{0:T(1024)}, f32[2048]{0:T(1024)S(1)}, u32[]{:S(2)}) copy-start(f32[2048]{0:T(1024)S(1)} %get-tuple-element.26) | copy-start | bytes 24580
  127.0 161.3 %copy-start.17 = (f32[2048]{0:T(1024)}, f32[2048]{0:T(1024)S(1)}, u32[]{:S(2)}) copy-start(f32[2048]{0:T(1024)S(1)} %fusion.91) | copy-start | bytes 24580
  145.6 33.5 %copy-start.10 = (bf16[1,2048,512]{2,1,0:T(8,128)(2,1)S(1)}, bf16[1,2048,512]{2,1,0:T(8,128)(2,1)}, u32[]{:S(2)}) copy-start(bf16[1,2048,512]{2,1,0:T(8,128)(2,1)} %param.12) | copy-start | bytes 6291460
  254.0 21.0 %copy-start.12 = (bf16[2048,512]{0,1:T(8,128)(2,1)S(1)}, bf16[2048,512]{0,1:T(8,128)(2,1)}, u32[]{:S(2)}) copy-start(bf16[2048,512]{0,1:T(8,128)(2,1)} %get-tuple-element.27) | copy-start | bytes 6291460
  254.0 21.0 %copy-start.21 = (bf16[1,512,4096]{2,1,0:T(8,128)(2,1)S(1)}, bf16[1,512,4096]{2,1,0:T(8,128)(2,1)}, u32[]{:S(2)}) copy-start(bf16[1,512,4096]{2,1,0:T(8,128)(2,1)} %all-gather.19.cloned.1.call-done) | copy-start | bytes 12582916
  274.9 13.3 %copy-start.16 = (f32[2048]{0:T(1024)S(1)}, f32[2048]{0:T(1024)}, u32[]{:S(2)}) copy-start(f32[2048]{0:T(1024)} %copy-done.15) | copy-start | bytes 24580
  275.0 13.4 %copy-start.6 = (bf16[1,2048,512]{1,2,0:T(8,128)(2,1)S(1)}, bf16[1,2048,512]{1,2,0:T(8,128)(2,1)}, u32[]{:S(2)}) copy-start(bf16[1,2048,512]{1,2,0:T(8,128)(2,1)} %copy.21) | copy-start | bytes 6291460
  289.7 1.3 copy-start.14
  305.0 1.6 copy-start.11
  305.0 135.6 %reduce-scatter.17.cloned.1.call-start = ((), (), s32[]{:S(2)}) async-start(), calls=%async_computation.11 | async-start | bytes 5242880 | tf_op jit(solution)/shard_map/reduce_scatter | solution.py:53
  332.6 15.3 %copy-start.5 = (bf16[1,2048,512]{1,2,0:T(8,128)(2,1)S(1)}, bf16[1,2048,512]{1,2,0:T(8,128)(2,1)}, u32[]{:S(2)}) copy-start(bf16[1,2048,512]{1,2,0:T(8,128)(2,1)} %copy-done.4) | copy-start | bytes 6291460
  332.6 15.3 %copy-start.20 = (f32[2048]{0:T(1024)S(1)}, f32[2048]{0:T(1024)}, u32[]{:S(2)}) copy-start(f32[2048]{0:T(1024)} %copy-done.19) | copy-start | bytes 24580
  332.7 111.4 %reduce-scatter.11.cloned.1.call-start = ((), (), s32[]{:S(2)}) async-start(), calls=%async_computation.8 | async-start | bytes 5242880 | tf_op jit(solution)/shard_map/reduce_scatter | solution.py:53
  369.5 0.7 copy-start.18
  369.5 97.9 %reduce-scatter.13.cloned.1.call-start = ((), (), s32[]{:S(2)}) async-start(), calls=%async_computation.9 | async-start | bytes 5242880 | tf_op jit(solution)/shard_map/reduce_scatter | solution.py:53
  392.5 116.3 %reduce-scatter.7.cloned.1.call-start = ((), (), s32[]{:S(2)}) async-start(), calls=%async_computation.6 | async-start | bytes 5242880 | tf_op jit(solution)/shard_map/reduce_scatter | solution.py:53
  425.0 1.6 copy-start.13
  425.0 125.0 %reduce-scatter.9.cloned.1.call-start = ((), (), s32[]{:S(2)}) async-start(), calls=%async_computation.7 | async-start | bytes 5242880 | tf_op jit(solution)/shard_map/reduce_scatter | solution.py:53
  440.6 121.6 %copy-start.1 = (bf16[2,1024,512]{2,1,0:T(8,128)(2,1)S(1)}, bf16[2,1024,512]{2,1,0:T(8,128)(2,1)}, u32[]{:S(2)}) copy-start(bf16[2,1024,512]{2,1,0:T(8,128)(2,1)} %param.15) | copy-start | bytes 6291460
  440.6 121.6 %copy-start.7 = (bf16[1024,512]{1,0:T(8,128)(2,1)S(1)}, bf16[1024,512]{1,0:T(8,128)(2,1)}, u32[]{:S(2)}) copy-start(bf16[1024,512]{1,0:T(8,128)(2,1)} %reduce-scatter.15.cloned.1.call-done) | copy-start | bytes 3145732
  562.2 8.1 %copy-start.2 = (bf16[2,128,4096]{2,1,0:T(8,128)(2,1)S(1)}, bf16[2,128,4096]{2,1,0:T(8,128)(2,1)}, u32[]{:S(2)}) copy-start(bf16[2,128,4096]{2,1,0:T(8,128)(2,1)} %param.13) | copy-start | bytes 6291460
  562.2 8.1 %copy-start.3 = (bf16[2,128,4096]{2,1,0:T(8,128)(2,1)S(1)}, bf16[2,128,4096]{2,1,0:T(8,128)(2,1)}, u32[]{:S(2)}) copy-start(bf16[2,128,4096]{2,1,0:T(8,128)(2,1)} %param.14) | copy-start | bytes 6291460
  562.2 8.1 %copy-start.8 = (bf16[128,4096]{1,0:T(8,128)(2,1)S(1)}, bf16[128,4096]{1,0:T(8,128)(2,1)}, u32[]{:S(2)}) copy-start(bf16[128,4096]{1,0:T(8,128)(2,1)} %reduce-scatter.11.cloned.1.call-done) | copy-start | bytes 3145732
  562.2 8.1 %copy-start.9 = (bf16[128,4096]{1,0:T(8,128)(2,1)S(1)}, bf16[128,4096]{1,0:T(8,128)(2,1)}, u32[]{:S(2)}) copy-start(bf16[128,4096]{1,0:T(8,128)(2,1)} %reduce-scatter.13.cloned.1.call-done) | copy-start | bytes 3145732
Sparse Core Ops, SparseCore 0:
  10.4 34.3 all-gather.12
  46.9 31.4 all-gather.14
  80.6 31.4 all-gather.16
  114.0 31.4 all-gather.22
  147.5 31.4 all-gather.20
  181.0 31.4 all-gather.18
  305.2 38.2 reduce-scatter.14
  346.5 38.2 reduce-scatter.16
  387.9 38.2 reduce-scatter.10
  429.1 38.2 reduce-scatter.12
  470.5 38.2 reduce-scatter.6
  511.7 38.2 reduce-scatter.8
where the time goes:
time: 599 us; the launch traced here: 591 us
  matrix products  317 us (53%)
  waiting for transfers between devices  196 us (33%)
  other arithmetic  33.2 us (6%)
  local copies, waits for them, and re-layouts  19.9 us (3%)
  between operations  17.6 us (3%)
  blocking collectives  6.27 us (1%)
    dot_general x5, matrix products, layer(): gate = jnp.dot(a, w['w_gate'], preferred_element_type=jnp.float32)  119 us
    dot_general x5, matrix products, layer(): up = jnp.dot(a, w['w_up'], preferred_element_type=jnp.float32)  115 us
    reduce_scatter x6, waiting for transfers between devices, step(): lax.psum_scatter(by_w[name], 'dp', scatter_dimension=0, tiled=True)  103 us
    all_gather x6, waiting for transfers between devices, fetched(): lax.all_gather(w[number], 'dp', axis=0, tiled=True)  91.6 us
    dot_general x5, matrix products, matmul(): jnp.dot(a, w, preferred_element_type=jnp.float32).astype(jnp.bfloat16)  84 us
    convert_element_type x2, other arithmetic, adamw(): return ((w - 0.02 * step).astype(jnp.bfloat16), m, v)  21.5 us
    unnamed x46, local copies, waits for them, and re-layouts  12.2 us
  transfers between devices with their start and end apart: 12, of which 9 were waited for; matrix products, arithmetic and copies ran while one was open for 42% of the time, Pallas kernels for 0%

commit v1 on v0

v1 whole, which is shorter than its diff:
```python
import functools

import jax
import jax.numpy as jnp
from jax import lax
from jax.experimental import pallas as pl
from jax.experimental.pallas import tpu as pltpu
from jax.sharding import PartitionSpec as P

MESH = pl.DeviceIdType.MESH
F32, BF16 = jnp.float32, jnp.bfloat16
T, D, FF = 2048, 512, 4096
CH = 8
B = 128
C = 4 * B
TT = 512
N = 2 * CH


def dot(a, b):
    return jnp.dot(a, b, preferred_element_type=F32)


def dot_nt(a, b):
    return lax.dot_general(a, b, (((1,), (1,)), ((), ())), preferred_element_type=F32)


def normed(h):
    wide = h.astype(F32)
    return (wide * lax.rsqrt(jnp.mean(wide * wide, -1, keepdims=True) + 1e-6)).astype(BF16)


def kernel(
    x_ref, dy_ref, wg_ref, wu_ref, wd_ref, gg_ref, gu_ref, gd_ref, sq_ref,
    W, A, H, AT, DY, DYT, ACC, PB, DG, DU, G, R, X, XR, SO, GB, SQ,
    own_s, xs, xr, ys, yr, ds, dr, es, er, rs, rr, zs, zr, ld, gs, credit,
):
    me, rep = lax.axis_index("dp"), lax.axis_index("rep")
    core, chip = lax.rem(me, 2), lax.div(me, 2)
    xp, mate = lax.rem(me + 2, 4), me + 1 - 2 * core
    matexp = lax.rem(mate + 2, 4)
    to_x, to_mate, to_y = {"dp": xp}, {"dp": mate}, {"rep": 1 - rep}
    half = pl.ds(pl.multiple_of(64 * rep, 64), 64)
    other_half = pl.ds(pl.multiple_of(64 * (1 - rep), 64), 64)

    barrier = pltpu.get_barrier_semaphore()
    for to in (to_x, to_mate, to_y):
        pl.semaphore_signal(barrier, inc=1, device_id=to, device_id_type=MESH)

    def split(n):
        return lax.div(n, CH), lax.rem(n, CH)

    def own(n, _):
        l, i = split(n)
        for d in range(4):
            cols = pl.ds(pl.multiple_of(1024 * d + B * i, B), B)
            pltpu.make_async_copy(wg_ref.at[l, :, cols], W.at[l, i, me, 0, :, pl.ds(B * d, B)], own_s.at[n]).start()
            pltpu.make_async_copy(wu_ref.at[l, :, cols], W.at[l, i, me, 1, :, pl.ds(B * d, B)], own_s.at[n]).start()
        pltpu.make_async_copy(wd_ref.at[l, pl.ds(pl.multiple_of(B * i, B), B), :], W.at[l, i, me, 2], own_s.at[n]).start()
        return 0

    lax.fori_loop(0, CH, own, 0)
    pltpu.make_async_copy(x_ref, A, ld.at[0]).start()
    pltpu.make_async_copy(dy_ref, DY, ld.at[1]).start()
    pltpu.make_async_copy(x_ref, H, ld.at[2]).start()
    lax.fori_loop(CH, N, own, 0)

    def remote(src, dst, s, r, to):
        return pltpu.make_async_remote_copy(src_ref=src, dst_ref=dst, send_sem=s, recv_sem=r, device_id=to, device_id_type=MESH)

    def move_x(n, block=None):
        l, i = split(n)
        ref = W.at[l, i, me if block is None else block, :, half, :]
        return remote(ref, ref, xs.at[n], xr.at[n], to_x)

    def move_y(n, which):
        l, i = split(n)
        ref = W.at[l, i, xp, :, which, :]
        return remote(ref, ref, ys.at[n], yr.at[n], to_y)

    def move_d(n, block):
        l, i = split(n)
        ref = W.at[l, i, block]
        return remote(ref, ref, ds.at[n], dr.at[n], to_mate)

    def move_e(n, block):
        l, i = split(n)
        ref = W.at[l, i, block]
        return remote(ref, ref, es.at[n], er.at[n], to_mate)

    pl.semaphore_wait(barrier, 3)

    def send_own(n, _):
        l, i = split(n)
        pltpu.make_async_copy(W.at[l, i, me], W.at[l, i, me], own_s.at[n]).wait()
        move_x(n).start()
        move_d(n, me).start()
        return 0

    lax.fori_loop(0, N, send_own, 0)

    def pump_x(n):
        move_x(n, xp).wait_recv()
        move_y(n, half).start()

    def pump_y(n):
        move_y(n, other_half).wait_recv()
        move_e(n, xp).start()

    def arrive(n):
        @pl.when(n + 2 < N)
        def _():
            pump_x(n + 2)

        @pl.when(n + 1 < N)
        def _():
            pump_y(n + 1)

        move_d(n, mate).wait_recv()
        move_e(n, matexp).wait_recv()

    def tiles(body):
        def one(t, _):
            body(pl.ds(pl.multiple_of(t * TT, TT), TT))
            return 0

        lax.fori_loop(0, T // TT, one, 0)

    def columns(t):
        return pl.ds(pl.multiple_of(t * TT, TT), TT)

    def transposed(src, dst):
        def one(t, _):
            dst[:, columns(t)] = src[columns(t), :].T
            return 0

        lax.fori_loop(0, T // TT, one, 0)

    pltpu.make_async_copy(x_ref, A, ld.at[0]).wait()

    def norm_a(rows):
        A[rows, :] = normed(A[rows, :])
        ACC[rows, :] = jnp.zeros((TT, D), F32)

    tiles(norm_a)
    pltpu.make_async_copy(dy_ref, DY, ld.at[1]).wait()
    transposed(DY, DYT)
    pltpu.make_async_copy(x_ref, H, ld.at[2]).wait()
    SQ[...] = jnp.zeros_like(SQ)

    pump_x(0)
    pump_x(1)
    pump_y(0)

    def matrix(l, i, which):
        return W[l, i, :, which].reshape(4 * B, 512)

    def forward(i, _):
        arrive(i)

        def tile(rows):
            a = A[rows, :]
            gate, up = dot(a, matrix(0, i, 0)), dot(a, matrix(0, i, 1))
            p = (gate * jax.nn.sigmoid(gate) * up).astype(BF16)
            ACC[rows, :] += dot(p, matrix(0, i, 2))

        tiles(tile)
        return 0

    lax.fori_loop(0, CH, forward, 0)

    def between(rows):
        h = (H[rows, :].astype(F32) + ACC[rows, :].astype(BF16).astype(F32)).astype(BF16)
        H[rows, :] = h
        A[rows, :] = normed(h)
        ACC[rows, :] = jnp.zeros((TT, D), F32)

    tiles(between)
    transposed(A, AT)

    def to_core(q):
        return remote(G.at[lax.rem(q, 2), 1 - core], R.at[lax.rem(q, 2)], rs.at[q], rr.at[q], to_mate)

    def to_chip(q):
        return remote(X.at[lax.rem(q, 3)], XR.at[lax.rem(q, 6)], zs.at[q], zr.at[q], to_x)

    def on_chip(q):
        slot = lax.rem(q, 2)
        to_core(q).wait_recv()

        @pl.when(q >= 3)
        def _():
            to_chip(q - 3).wait_send()

        for j in range(3):
            X[lax.rem(q, 3), j] = (G[slot, core, 1 - chip, j].astype(F32) + R[slot, 1 - chip, j].astype(F32)).astype(BF16)
            SO[lax.rem(q, 3), j] = G[slot, core, chip, j].astype(F32) + R[slot, chip, j].astype(F32)

        @pl.when(q >= 6)
        def _():
            pl.semaphore_wait(credit, 1)

        to_chip(q).start()

    def put(q, slot):
        l, i = 1 - lax.div(q, CH), lax.rem(q, CH)
        for d in range(4):
            cols = pl.ds(pl.multiple_of(1024 * d + B * i, B), B)
            pltpu.make_async_copy(GB.at[slot, 0, :, pl.ds(B * d, B)], gg_ref.at[l, :, cols], gs.at[slot]).start()
            pltpu.make_async_copy(GB.at[slot, 1, :, pl.ds(B * d, B)], gu_ref.at[l, :, cols], gs.at[slot]).start()
        pltpu.make_async_copy(GB.at[slot, 2], gd_ref.at[l, pl.ds(pl.multiple_of(B * i, B), B), :], gs.at[slot]).start()

    def put_wait(slot):
        pltpu.make_async_copy(GB.at[slot], GB.at[slot], gs.at[slot]).wait()

    def final(q):
        slot = lax.rem(q, 2)
        to_chip(q).wait_recv()

        @pl.when(q >= 2)
        def _():
            put_wait(slot)

        for j in range(3):
            g = (SO[lax.rem(q, 3), j] + XR[lax.rem(q, 6), j].astype(F32)).astype(BF16)
            GB[slot, j] = g
            wide = g.astype(F32)
            SQ[...] += jnp.sum((wide * wide).reshape(B // 8, 8, 512), axis=0)

        @pl.when(q < N - 6)
        def _():
            pl.semaphore_signal(credit, inc=1, device_id=to_x, device_id_type=MESH)

        put(q, slot)

    def backward(q, i, l):
        def tile(rows):
            a, by = A[rows, :], DY[rows, :]
            wg, wu = matrix(l, i, 0), matrix(l, i, 1)
            gate, up = dot(a, wg), dot(a, wu)
            dp = dot_nt(by, matrix(l, i, 2)).astype(BF16).astype(F32)
            s = jax.nn.sigmoid(gate)
            silu = gate * s
            PB[rows, :] = (silu * up).astype(BF16)
            du = (dp * silu).astype(BF16)
            dg = (dp * up * (s + silu * (1.0 - s))).astype(BF16)
            DU[rows, :] = du
            DG[rows, :] = dg
            if l == 1:
                ACC[rows, :] += dot_nt(dg, wg) + dot_nt(du, wu)

        tiles(tile)

        @pl.when(q >= 4)
        def _():
            final(q - 4)

        @pl.when(q >= 1)
        def _():
            on_chip(q - 1)

        @pl.when(q >= 2)
        def _():
            to_core(q - 2).wait_send()

        slot = lax.rem(q, 2)
        for j, made in enumerate((lambda: dot(AT[...], DG[...]), lambda: dot(AT[...], DU[...]), lambda: dot(DYT[...], PB[...]).T)):
            by_w = made().astype(BF16)
            for d in range(4):
                G[slot, d % 2, d // 2, j] = by_w[B * d : B * (d + 1)]
        to_core(q).start()

    def last_layer(i, _):
        arrive(CH + i)
        backward(i, i, 1)
        return 0

    lax.fori_loop(0, CH, last_layer, 0)

    again = pltpu.make_async_copy(x_ref, A, ld.at[0])
    again.start()

    def norm_back(rows):
        h, da = H[rows, :].astype(F32), ACC[rows, :].astype(BF16).astype(F32)
        scale = lax.rsqrt(jnp.mean(h * h, -1, keepdims=True) + 1e-6)
        inner = jnp.sum(da * h, -1, keepdims=True)
        by_h = da * scale - h * (inner * scale * scale * scale * (1.0 / D))
        DY[rows, :] = (DY[rows, :].astype(F32) + by_h.astype(BF16).astype(F32)).astype(BF16)

    tiles(norm_back)
    transposed(DY, DYT)
    again.wait()

    def norm_again(rows):
        A[rows, :] = normed(A[rows, :])

    tiles(norm_again)
    transposed(A, AT)

    def first_layer(i, _):
        backward(CH + i, i, 0)
        return 0

    lax.fori_loop(0, CH, first_layer, 0)

    final(N - 4)
    on_chip(N - 1)
    for q in range(N - 3, N):
        final(q)
    sq_ref[...] = SQ[...]
    put_wait(0)
    put_wait(1)

    def drain(n, _):
        move_x(n).wait_send()
        move_y(n, half).wait_send()
        move_d(n, me).wait_send()
        move_e(n, xp).wait_send()
        return 0

    lax.fori_loop(0, N, drain, 0)
    for q in range(N - 2, N):
        to_core(q).wait_send()
    for q in range(N - 3, N):
        to_chip(q).wait_send()


def gradients(x, dy, wg, wu, wd):
    any_space, vmem = pl.BlockSpec(memory_space=pl.ANY), pl.BlockSpec(memory_space=pltpu.VMEM)
    sems = [pltpu.SemaphoreType.DMA((N,))] * 13 + [pltpu.SemaphoreType.DMA((3,)), pltpu.SemaphoreType.DMA((2,)), pltpu.SemaphoreType.REGULAR]
    block = (3, B, 512)
    return pl.pallas_call(
        kernel,
        out_shape=(
            jax.ShapeDtypeStruct(wg.shape, BF16),
            jax.ShapeDtypeStruct(wu.shape, BF16),
            jax.ShapeDtypeStruct(wd.shape, BF16),
            jax.ShapeDtypeStruct((8, 512), F32),
        ),
        in_specs=[any_space] * 5,
        out_specs=(any_space, any_space, any_space, vmem),
        scratch_shapes=[
            pltpu.VMEM((2, CH, 4) + block, BF16),
            pltpu.VMEM((T, D), BF16),
            pltpu.VMEM((T, D), BF16),
            pltpu.VMEM((D, T), BF16),
            pltpu.VMEM((T, D), BF16),
            pltpu.VMEM((D, T), BF16),
            pltpu.VMEM((T, D), F32),
            pltpu.VMEM((T, C), BF16),
            pltpu.VMEM((T, C), BF16),
            pltpu.VMEM((T, C), BF16),
            pltpu.VMEM((2, 2, 2) + block, BF16),
            pltpu.VMEM((2, 2) + block, BF16),
            pltpu.VMEM((3,) + block, BF16),
            pltpu.VMEM((6,) + block, BF16),
            pltpu.VMEM((3,) + block, F32),
            pltpu.VMEM((2,) + block, BF16),
            pltpu.VMEM((8, 512), F32),
        ]
        + sems,
        compiler_params=pltpu.CompilerParams(collective_id=0, has_side_effects=True, vmem_limit_bytes=67043328),
        name="step",
    )(x, dy, wg, wu, wd)


def adamw(w, m, v, g):
    m = 0.9 * m + 0.1 * g
    v = 0.95 * v + 0.05 * g * g
    step = m * lax.rsqrt(v + 1e-8) + 0.1 * w
    return (w - 0.02 * step).astype(BF16), m, v


def solution(mesh):
    def step(x, dy, *arrays):
        weights, m, v = (arrays[i : i + 3] for i in (0, 3, 6))
        *grads, squares = gradients(x[0], dy[0], *weights)
        total = lax.psum(jnp.sum(squares), "dp")
        count = 4 * sum(g.size for g in grads)
        factor = jnp.minimum(1.0, 0.5 * lax.rsqrt(total / count + 1e-30))
        new = [adamw(w.astype(F32), m, v, g.astype(F32) * factor) for w, m, v, g in zip(weights, m, v, grads, strict=True)]
        return tuple(one[which] for which in range(3) for one in new)

    states, cut = P(("rep", "dp"), None, None), P(None, "dp", None)
    return jax.shard_map(
        step,
        mesh=mesh,
        in_specs=(states, states) + (cut,) * 9,
        out_specs=(P("rep", "dp", None),) * 9,
        check_vma=False,
    )
```

time: 599 us -> 272 us (0.45); the launches traced: 591 us -> 272 us
  matrix products: 317 us -> 0 us
  Pallas kernels: 0 us -> 238 us
  waiting for transfers between devices: 196 us -> 0 us
  local copies, waits for them, and re-layouts: 19.9 us -> 0.02 us
  between operations: 17.6 us -> 1.4 us
  other arithmetic: 33.2 us -> 25 us
    dot_general x15 -> x0, matrix products: 317 us -> none  [the longest x5 119 us: layer(): gate = jnp.dot(a, w['w_gate'], preferred_element_type=jnp.float32)]
    pallas_call x0 -> x1, Pallas kernels: none -> 238 us  [gradients(): pl.pallas_call(kernel, out_shape=(jax.ShapeDtypeStruct(wg.shape, BF16), j...]
    reduce_scatter x6 -> x0, waiting for transfers between devices: 103 us -> none  [step(): lax.psum_scatter(by_w[name], 'dp', scatter_dimension=0, tiled=True)]
    all_gather x6 -> x0, waiting for transfers between devices: 91.6 us -> none  [fetched(): lax.all_gather(w[number], 'dp', axis=0, tiled=True)]
    unnamed x46 -> x6, local copies, waits for them, and re-layouts: 12.2 us -> 0.02 us
    reduce_sum x4 -> x1, other arithmetic: 10.3 us -> 1.33 us  [step(): total = lax.psum(jnp.sum(squares), 'dp')]
    slice x3 -> x0, local copies, waits for them, and re-layouts: 7.74 us -> none  [fetched(): w[number]]
  transfers between devices with their start and end apart: 12 -> 0, of which waited for: 9 -> 0; matrix products, arithmetic and copies ran while one was open for 42% -> 0% of each run, Pallas kernels for 0% -> 0%
where the time goes in v1:
time: 272 us
  Pallas kernels  238 us (88%)
  other arithmetic  25 us (9%)
  blocking collectives  7.7 us (3%)
    pallas_call x1, Pallas kernels, gradients(): pl.pallas_call(kernel, out_shape=(jax.ShapeDtypeStruct(wg.shape, BF16), j...  238 us
    convert_element_type x2, other arithmetic, adamw(): return ((w - 0.02 * step).astype(BF16), m, v)  23.6 us
    psum x1, blocking collectives, step(): total = lax.psum(jnp.sum(squares), 'dp')  7.7 us

profile of v1, /device:TPU:0, one launch (start us, length us, event | category | flops | bytes accessed | tf_op | source)
XLA Modules:
  0.0 272.1 jit_solution(7527790891856529593)
XLA Ops:
  0.6 238.0 %step.1 = (bf16[2,128,4096]{2,1,0:T(8,128)(2,1)}, bf16[2,128,4096]{2,1,0:T(8,128)(2,1)}, bf16[2,1024,512]{2,1,0:T(8,128)(2,1)}, f32[8,512]{1,0:T(8,128)}) custom-call(bf16[2048,512]{1,0:T(8,128)(2,1)} %bitcast.2, bf16[2048,512]{1,0:T(8,128)(2,1)} %bitcast.3, bf16[2,128,4096]{2,1,0:T(8,128)(2,1)} %wg_ref.1, bf16[2,128,4096]{2,1,0:T(8,128)(2,1)} %wu_ref.1, ...), custom_call_target="tpu_custom_call" | custom-call | tf_op jit(solution)/shard_map/step/pallas_call | solution.py:332
  238.6 1.3 reduce_sum.9
  240.0 7.7 %psum.7 = f32[]{:T(128)} all-reduce(f32[]{:T(128)} %reduce_sum.9), channel_id=1, replica_groups=mesh['rep'=2,'dp'=4] {'dp'}, use_global_device_ids=true, to_apply=%region_1.0 | all-reduce | flops 1 | bytes 8 | tf_op jit(solution)/shard_map/psum | solution.py:378
  248.4 0.0 copy-start
  248.4 0.0 copy-start.1
  248.4 0.0 copy-start.2
  248.4 17.4 %fusion.2 = (bf16[2,128,4096]{2,1,0:T(8,128)(2,1)}, f32[2,128,4096]{2,1,0:T(8,128)}, f32[2,128,4096]{2,1,0:T(8,128)}, bf16[2,128,4096]{2,1,0:T(8,128)(2,1)}, f32...) fusion(bf16[2,128,4096]{2,1,0:T(8,128)(2,1)} %wg_ref.1, f32[]{:T(128)S(6)} %min_shard_map.3, ...), kind=kLoop, calls=%fused_computation.11 | loop fusion | flops 35651584 | bytes 46137348 | tf_op jit(solution)/shard_map/convert_element_type | solution.py:371
  265.8 0.0 copy-done
  265.8 0.0 copy-done.1
  265.8 0.0 copy-done.2
  265.8 6.2 %fusion.8 = (bf16[2,1024,512]{2,1,0:T(8,128)(2,1)}, f32[2,1024,512]{2,1,0:T(8,128)}, f32[2,1024,512]{2,1,0:T(8,128)}) fusion(bf16[2,1024,512]{2,1,0:T(8,128)(2,1)S(1)} %copy-done, f32[]{:T(128)S(6)} %min_shard_map.3, bf16[2,1024,512]{2,1,0:T(8,128)(2,1)S(1)} %copy-done.2, f32[2,1024,512]{2,1,0:T(8,128)S(1)} %copy-done.1, f32[2,1024,512]{2,1,0:T(8,128)} %param.18), kind=kLoop, calls=%fused_computation.17 | loop fusion | flops 17825792 | bytes 23068676 | tf_op jit(solution)/shard_map/convert_element_type | solution.py:371
Async XLA Ops:
  248.4 17.5 %copy-start = (bf16[2,1024,512]{2,1,0:T(8,128)(2,1)S(1)}, bf16[2,1024,512]{2,1,0:T(8,128)(2,1)}, u32[]{:S(2)}) copy-start(bf16[2,1024,512]{2,1,0:T(8,128)(2,1)} %wd_ref.1) | copy-start | bytes 6291460
  248.4 17.4 %copy-start.1 = (f32[2,1024,512]{2,1,0:T(8,128)S(1)}, f32[2,1024,512]{2,1,0:T(8,128)}, u32[]{:S(2)}) copy-start(f32[2,1024,512]{2,1,0:T(8,128)} %param.21) | copy-start | bytes 12582916
  248.4 17.4 %copy-start.2 = (bf16[2,1024,512]{2,1,0:T(8,128)(2,1)S(1)}, bf16[2,1024,512]{2,1,0:T(8,128)(2,1)}, u32[]{:S(2)}) copy-start(bf16[2,1024,512]{2,1,0:T(8,128)(2,1)} %get-tuple-element.16) | copy-start | bytes 6291460

commit v2 on v1

v2 whole, which is shorter than its diff:
```python
import functools

import jax
import jax.numpy as jnp
from jax import lax
from jax.experimental import pallas as pl
from jax.experimental.pallas import tpu as pltpu
from jax.sharding import PartitionSpec as P

MESH = pl.DeviceIdType.MESH
F32, BF16 = jnp.float32, jnp.bfloat16
T, D, FF = 2048, 512, 4096
CH = 8
B = 128
C = 4 * B
TT = 512
N = 2 * CH


def dot(a, b):
    return jnp.dot(a, b, preferred_element_type=F32)


def dot_nt(a, b):
    return lax.dot_general(a, b, (((1,), (1,)), ((), ())), preferred_element_type=F32)


def normed(h):
    wide = h.astype(F32)
    return (wide * lax.rsqrt(jnp.mean(wide * wide, -1, keepdims=True) + 1e-6)).astype(BF16)


def kernel(
    x_ref, dy_ref, wg_ref, wu_ref, wd_ref, gg_ref, gu_ref, gd_ref, sq_ref,
    W, A0, A0T, A1, A1T, H, DY, DYT, ACC, PB0, PB1, DG0, DG1, DU0, DU1, AW, G, R, X, XR, SO, GB, SQ, S, SR,
    xs, xr, ys, yr, es, er, own_s, ds, dr, rs, rr, zs, zr, ld, gs, ss, sr, credit,
):
    me, rep = lax.axis_index("dp"), lax.axis_index("rep")
    core, chip = lax.rem(me, 2), lax.div(me, 2)
    xp, mate = lax.rem(me + 2, 4), me + 1 - 2 * core
    matexp = lax.rem(mate + 2, 4)
    to_x, to_mate, to_y = {"dp": xp}, {"dp": mate}, {"rep": 1 - rep}
    half = pl.ds(pl.multiple_of(64 * rep, 64), 64)
    other_half = pl.ds(pl.multiple_of(64 * (1 - rep), 64), 64)

    barrier = pltpu.get_barrier_semaphore()
    for to in (to_x, to_mate, to_y):
        pl.semaphore_signal(barrier, inc=1, device_id=to, device_id_type=MESH)

    def split(n):
        return lax.div(n, CH), lax.rem(n, CH)

    def own(n, _):
        l, i = split(n)
        for d in range(4):
            cols = pl.ds(pl.multiple_of(1024 * d + B * i, B), B)
            pltpu.make_async_copy(wg_ref.at[l, :, cols], W.at[l, i, me, 0, :, pl.ds(B * d, B)], own_s.at[n]).start()
            pltpu.make_async_copy(wu_ref.at[l, :, cols], W.at[l, i, me, 1, :, pl.ds(B * d, B)], own_s.at[n]).start()
        pltpu.make_async_copy(wd_ref.at[l, pl.ds(pl.multiple_of(B * i, B), B), :], W.at[l, i, me, 2], own_s.at[n]).start()
        return 0

    lax.fori_loop(0, CH, own, 0)
    pltpu.make_async_copy(x_ref, A0, ld.at[0]).start()
    pltpu.make_async_copy(dy_ref, DY, ld.at[1]).start()
    pltpu.make_async_copy(x_ref, H, ld.at[2]).start()
    lax.fori_loop(CH, N, own, 0)

    def remote(src, dst, s, r, to):
        return pltpu.make_async_remote_copy(src_ref=src, dst_ref=dst, send_sem=s, recv_sem=r, device_id=to, device_id_type=MESH)

    def piece(u):
        n = lax.div(u, 3)
        return split(n) + (lax.rem(u, 3),)

    def move_x(u, block=None):
        l, i, j = piece(u)
        ref = W.at[l, i, me if block is None else block, j, half, :]
        return remote(ref, ref, xs.at[u], xr.at[u], to_x)

    def move_y(u, which):
        l, i, j = piece(u)
        ref = W.at[l, i, xp, j, which, :]
        return remote(ref, ref, ys.at[u], yr.at[u], to_y)

    def move_e(u, block):
        l, i, j = piece(u)
        ref = W.at[l, i, block, j]
        return remote(ref, ref, es.at[u], er.at[u], to_mate)

    def move_d(n, block):
        l, i = split(n)
        ref = W.at[l, i, block]
        return remote(ref, ref, ds.at[n], dr.at[n], to_mate)

    pl.semaphore_wait(barrier, 3)

    def send_own(n, _):
        l, i = split(n)
        pltpu.make_async_copy(W.at[l, i, me], W.at[l, i, me], own_s.at[n]).wait()
        for j in range(3):
            move_x(3 * n + j).start()
        move_d(n, me).start()
        return 0

    lax.fori_loop(0, N, send_own, 0)

    def pump_x(u):
        move_x(u, xp).wait_recv()
        move_y(u, half).start()

    def pump_y(u):
        move_y(u, other_half).wait_recv()
        move_e(u, xp).start()

    def arrive(n):
        move_d(n, mate).wait_recv()
        for j in range(3):
            move_e(3 * n + j, matexp).wait_recv()

    def tiles(body):
        def one(t, _):
            body(pl.ds(pl.multiple_of(t * TT, TT), TT))
            return 0

        lax.fori_loop(0, T // TT, one, 0)

    def columns(t):
        return pl.ds(pl.multiple_of(t * TT, TT), TT)

    def transposed(src, dst):
        def one(t, _):
            dst[:, columns(t)] = src[columns(t), :].T
            return 0

        lax.fori_loop(0, T // TT, one, 0)

    pltpu.make_async_copy(x_ref, A0, ld.at[0]).wait()

    def norm_a(rows):
        A0[rows, :] = normed(A0[rows, :])
        ACC[rows, :] = jnp.zeros((TT, D), F32)

    tiles(norm_a)
    pump_x(0)
    pump_x(1)
    pltpu.make_async_copy(dy_ref, DY, ld.at[1]).wait()
    transposed(DY, DYT)
    pump_x(2)
    pump_y(0)
    pltpu.make_async_copy(x_ref, H, ld.at[2]).wait()
    transposed(A0, A0T)
    SQ[...] = jnp.zeros_like(SQ)
    pump_x(3)
    pump_y(1)
    pump_x(4)
    pump_y(2)

    def matrix(l, i, which):
        return W[l, i, :, which].reshape(4 * B, 512)

    def forward(i, _):
        arrive(i)
        for t in range(T // TT):
            if t > 0:
                pump_x(3 * i + t + 4)
                pump_y(3 * i + t + 2)
            rows = slice(t * TT, (t + 1) * TT)
            a = A0[rows, :]
            gate, up = dot(a, matrix(0, i, 0)), dot(a, matrix(0, i, 1))
            p = (gate * jax.nn.sigmoid(gate) * up).astype(BF16)
            ACC[rows, :] += dot(p, matrix(0, i, 2))
        return 0

    lax.fori_loop(0, CH, forward, 0)

    def between(rows):
        h = (H[rows, :].astype(F32) + ACC[rows, :].astype(BF16).astype(F32)).astype(BF16)
        H[rows, :] = h
        A1[rows, :] = normed(h)
        ACC[rows, :] = jnp.zeros((TT, D), F32)

    tiles(between)
    transposed(A1, A1T)

    def to_core(q):
        return remote(G.at[lax.rem(q, 2), 1 - core], R.at[lax.rem(q, 2)], rs.at[q], rr.at[q], to_mate)

    def to_chip(q):
        return remote(X.at[lax.rem(q, 3)], XR.at[lax.rem(q, 6)], zs.at[q], zr.at[q], to_x)

    def on_chip(q):
        slot = lax.rem(q, 2)
        to_core(q).wait_recv()

        @pl.when(q >= 3)
        def _():
            to_chip(q - 3).wait_send()

        for j in range(3):
            X[lax.rem(q, 3), j] = (G[slot, core, 1 - chip, j].astype(F32) + R[slot, 1 - chip, j].astype(F32)).astype(BF16)
            SO[lax.rem(q, 4), j] = G[slot, core, chip, j].astype(F32) + R[slot, chip, j].astype(F32)

        @pl.when(q >= 6)
        def _():
            pl.semaphore_wait(credit, 1)

        to_chip(q).start()

    def put(q, slot):
        l, i = 1 - lax.div(q, CH), lax.rem(q, CH)
        for d in range(4):
            cols = pl.ds(pl.multiple_of(1024 * d + B * i, B), B)
            pltpu.make_async_copy(GB.at[slot, 0, :, pl.ds(B * d, B)], gg_ref.at[l, :, cols], gs.at[slot]).start()
            pltpu.make_async_copy(GB.at[slot, 1, :, pl.ds(B * d, B)], gu_ref.at[l, :, cols], gs.at[slot]).start()
        pltpu.make_async_copy(GB.at[slot, 2], gd_ref.at[l, pl.ds(pl.multiple_of(B * i, B), B), :], gs.at[slot]).start()

    def put_wait(slot):
        pltpu.make_async_copy(GB.at[slot], GB.at[slot], gs.at[slot]).wait()

    def final(q):
        slot = lax.rem(q, 2)
        to_chip(q).wait_recv()

        @pl.when(q >= 2)
        def _():
            put_wait(slot)

        for j in range(3):
            g = (SO[lax.rem(q, 4), j] + XR[lax.rem(q, 6), j].astype(F32)).astype(BF16)
            GB[slot, j] = g
            wide = g.astype(F32)
            SQ[...] += jnp.sum((wide * wide).reshape(B // 8, 8, 512), axis=0)

        @pl.when(q < N - 6)
        def _():
            pl.semaphore_signal(credit, inc=1, device_id=to_x, device_id_type=MESH)

        put(q, slot)

    PB, DG, DU = (PB0, PB1), (DG0, DG1), (DU0, DU1)

    def tokens(n):
        return pl.ds(pl.multiple_of(lax.rem(n, 4) * TT, TT), TT)

    def first_half(n, slot, l, h):
        i, rows, cols = lax.div(n, 4), tokens(n), slice(256 * h, 256 * (h + 1))
        a, by = (A0, A1)[l][rows, :], DY[rows, :]
        gate = dot(a, W[l, i, :, 0, :, cols].reshape(D, 256))
        up = dot(a, W[l, i, :, 1, :, cols].reshape(D, 256))
        dp = dot_nt(by, W[l, i, 2 * h : 2 * h + 2, 2].reshape(256, D)).astype(BF16).astype(F32)
        s = jax.nn.sigmoid(gate)
        silu = gate * s
        PB[slot][:, cols] = (silu * up).astype(BF16)
        DU[slot][:, cols] = (dp * silu).astype(BF16)
        DG[slot][:, cols] = (dp * up * (s + silu * (1.0 - s))).astype(BF16)

    def by_input(n, slot, l):
        if l == 1:
            i, rows = lax.div(n, 4), tokens(n)
            ACC[rows, :] += dot_nt(DG[slot][...], matrix(l, i, 0)) + dot_nt(DU[slot][...], matrix(l, i, 1))

    def by_weight(n, slot, l, j):
        left = (A0T, A1T)[l] if j < 2 else DYT
        right = (DG, DU, PB)[j][slot]
        new = dot(left[:, tokens(n)], right[...])
        AW[j] = jnp.where(lax.rem(n, 4) == 0, 0.0, AW[j]) + new

    def both(n, slot, l):
        first_half(n + 1, 1 - slot, l, 0)
        by_input(n, slot, l)
        if l == 0:
            by_weight(n, slot, l, 0)
        first_half(n + 1, 1 - slot, l, 1)
        for j in range(1 - l, 3):
            by_weight(n, slot, l, j)

    def second(n, slot, l):
        by_input(n, slot, l)
        for j in range(3):
            by_weight(n, slot, l, j)

    def emit(q):
        @pl.when(q >= 2)
        def _():
            to_core(q - 2).wait_send()

        slot = lax.rem(q, 2)
        for j in range(3):
            by_w = AW[j].T.astype(BF16) if j == 2 else AW[j].astype(BF16)
            for d in range(4):
                G[slot, d % 2, d // 2, j] = by_w[B * d : B * (d + 1)]
        to_core(q).start()

    def sums(q):
        @pl.when(q >= 4)
        def _():
            final(q - 4)

        @pl.when((q >= 1) & (q != CH) & (q != CH + 1))
        def _():
            on_chip(q - 1)

    PAIRS = 2 * CH

    def layer_back(l):
        q0 = CH * (1 - l)

        def pair(j, _):
            i = lax.div(j, 2)
            if l == 1:
                for k in range(3):

                    @pl.when((26 + 3 * j + k >= 27) & (26 + 3 * j + k < 3 * N))
                    def _():
                        pump_y(26 + 3 * j + k)

                for k in range(3):

                    @pl.when(29 + 3 * j + k < 3 * N)
                    def _():
                        pump_x(29 + 3 * j + k)

                @pl.when(lax.rem(j, 2) == 1)
                def _():
                    arrive(CH + i + 1)

            both(2 * j, 0, l)
            both(2 * j + 1, 1, l)

            @pl.when(lax.rem(j, 2) == 0)
            def _():
                sums(q0 + i)

            @pl.when(lax.rem(j, 2) == 1)
            def _():
                emit(q0 + i)
                if l == 0:

                    @pl.when(i == 0)
                    def _():
                        on_chip(CH)

            return 0

        if l == 1:
            arrive(CH)
        for h in range(2):
            first_half(0, 0, l, h)
        lax.fori_loop(0, PAIRS - 1, pair, 0)
        both(2 * PAIRS - 2, 0, l)
        second(2 * PAIRS - 1, 1, l)
        emit(q0 + CH - 1)

    layer_back(1)

    def norm_back(rows):
        h, da = H[rows, :].astype(F32), ACC[rows, :].astype(BF16).astype(F32)
        scale = lax.rsqrt(jnp.mean(h * h, -1, keepdims=True) + 1e-6)
        inner = jnp.sum(da * h, -1, keepdims=True)
        by_h = da * scale - h * (inner * scale * scale * scale * (1.0 / D))
        DY[rows, :] = (DY[rows, :].astype(F32) + by_h.astype(BF16).astype(F32)).astype(BF16)

    tiles(norm_back)
    on_chip(CH - 1)
    transposed(DY, DYT)

    layer_back(0)

    on_chip(N - 1)
    for q in range(N - 4, N):
        final(q)

    S[0] = SQ[:, 0:128] + SQ[:, 128:256] + SQ[:, 256:384] + SQ[:, 384:512]
    put_wait(0)
    put_wait(1)

    def drain(u, _):
        move_x(u).wait_send()
        move_y(u, half).wait_send()
        move_e(u, xp).wait_send()
        return 0

    lax.fori_loop(0, 3 * N, drain, 0)

    def share(k, to):
        move = remote(S.at[k], SR.at[k], ss.at[k], sr.at[k], to)
        move.start()
        move.wait()

    share(0, to_mate)
    S[1] = S[0] + SR[0]

    def drain_d(n, _):
        move_d(n, me).wait_send()
        return 0

    lax.fori_loop(0, N, drain_d, 0)
    for q in range(N - 2, N):
        to_core(q).wait_send()
    for q in range(N - 3, N):
        to_chip(q).wait_send()
    share(1, to_x)
    sq_ref[...] = S[1] + SR[1]


def gradients(x, dy, wg, wu, wd):
    any_space, vmem = pl.BlockSpec(memory_space=pl.ANY), pl.BlockSpec(memory_space=pltpu.VMEM)
    sem = pltpu.SemaphoreType.DMA
    sems = [sem((3 * N,))] * 6 + [sem((N,))] * 7 + [sem((3,)), sem((2,)), sem((2,)), sem((2,)), pltpu.SemaphoreType.REGULAR]
    block = (3, B, 512)
    return pl.pallas_call(
        kernel,
        out_shape=(
            jax.ShapeDtypeStruct(wg.shape, BF16),
            jax.ShapeDtypeStruct(wu.shape, BF16),
            jax.ShapeDtypeStruct(wd.shape, BF16),
            jax.ShapeDtypeStruct((8, 128), F32),
        ),
        in_specs=[any_space] * 5,
        out_specs=(any_space, any_space, any_space, vmem),
        scratch_shapes=[
            pltpu.VMEM((2, CH, 4) + block, BF16),
            pltpu.VMEM((T, D), BF16),
            pltpu.VMEM((D, T), BF16),
            pltpu.VMEM((T, D), BF16),
            pltpu.VMEM((D, T), BF16),
            pltpu.VMEM((T, D), BF16),
            pltpu.VMEM((T, D), BF16),
            pltpu.VMEM((D, T), BF16),
            pltpu.VMEM((T, D), F32),
        ]
        + [pltpu.VMEM((TT, C), BF16)] * 6
        + [
            pltpu.VMEM((3, 512, 512), F32),
            pltpu.VMEM((2, 2, 2) + block, BF16),
            pltpu.VMEM((2, 2) + block, BF16),
            pltpu.VMEM((3,) + block, BF16),
            pltpu.VMEM((6,) + block, BF16),
            pltpu.VMEM((4,) + block, F32),
            pltpu.VMEM((2,) + block, BF16),
            pltpu.VMEM((8, 512), F32),
            pltpu.VMEM((2, 8, 128), F32),
            pltpu.VMEM((2, 8, 128), F32),
        ]
        + sems,
        compiler_params=pltpu.CompilerParams(collective_id=0, has_side_effects=True, vmem_limit_bytes=67043328),
        name="step",
    )(x, dy, wg, wu, wd)


def adamw(w, m, v, g):
    m = 0.9 * m + 0.1 * g
    v = 0.95 * v + 0.05 * g * g
    step = m * lax.rsqrt(v + 1e-8) + 0.1 * w
    return (w - 0.02 * step).astype(BF16), m, v


def solution(mesh):
    def step(x, dy, *arrays):
        weights, m, v = (arrays[i : i + 3] for i in (0, 3, 6))
        *grads, squares = gradients(x[0], dy[0], *weights)
        total = jnp.sum(squares)
        count = 4 * sum(g.size for g in grads)
        factor = jnp.minimum(1.0, 0.5 * lax.rsqrt(total / count + 1e-30))
        new = [adamw(w.astype(F32), m, v, g.astype(F32) * factor) for w, m, v, g in zip(weights, m, v, grads, strict=True)]
        return tuple(one[which] for which in range(3) for one in new)

    states, cut = P(("rep", "dp"), None, None), P(None, "dp", None)
    return jax.shard_map(
        step,
        mesh=mesh,
        in_specs=(states, states) + (cut,) * 9,
        out_specs=(P("rep", "dp", None),) * 9,
        check_vma=False,
    )
```

time: 272 us -> 272 us (level)
  Pallas kernels: 238 us -> 246 us
  blocking collectives: 7.7 us -> 0 us
    pallas_call x1, Pallas kernels: 238 us -> 246 us  [gradients(): pl.pallas_call(kernel, out_shape=(jax.ShapeDtypeStruct(wg.shape, BF16), j...]
    psum x1 -> x0, blocking collectives: 7.7 us -> none  [step(): total = lax.psum(jnp.sum(squares), 'dp')]
where the time goes in v2:
time: 272 us
  Pallas kernels  246 us (90%)
  other arithmetic  24.9 us (9%)
    pallas_call x1, Pallas kernels, gradients(): pl.pallas_call(kernel, out_shape=(jax.ShapeDtypeStruct(wg.shape, BF16), j...  246 us
    convert_element_type x2, other arithmetic, adamw(): return ((w - 0.02 * step).astype(BF16), m, v)  23.6 us

profile of v2, /device:TPU:0, one launch (start us, length us, event | category | flops | bytes accessed | tf_op | source)
XLA Modules:
  0.0 272.1 jit_solution(15620999311283761897)
XLA Ops:
  0.6 245.8 %step.1 = (bf16[2,128,4096]{2,1,0:T(8,128)(2,1)}, bf16[2,128,4096]{2,1,0:T(8,128)(2,1)}, bf16[2,1024,512]{2,1,0:T(8,128)(2,1)}, f32[8,128]{1,0:T(8,128)}) custom-call(bf16[2048,512]{1,0:T(8,128)(2,1)} %bitcast.2, bf16[2048,512]{1,0:T(8,128)(2,1)} %bitcast.3, bf16[2,128,4096]{2,1,0:T(8,128)(2,1)} %wg_ref.1, bf16[2,128,4096]{2,1,0:T(8,128)(2,1)} %wu_ref.1, ...), custom_call_target="tpu_custom_call" | custom-call | tf_op jit(solution)/shard_map/step/pallas_call | solution.py:411
  246.4 1.3 reduce_sum.9
  248.4 0.0 copy-start
  248.4 0.0 copy-start.1
  248.4 0.0 copy-start.2
  248.4 17.4 %fusion.2 = (bf16[2,128,4096]{2,1,0:T(8,128)(2,1)}, f32[2,128,4096]{2,1,0:T(8,128)}, f32[2,128,4096]{2,1,0:T(8,128)}, bf16[2,128,4096]{2,1,0:T(8,128)(2,1)}, f32...) fusion(bf16[2,128,4096]{2,1,0:T(8,128)(2,1)} %wg_ref.1, f32[]{:T(128)S(6)} %min_shard_map.3, ...), kind=kLoop, calls=%fused_computation.11 | loop fusion | flops 35651584 | bytes 46137348 | tf_op jit(solution)/shard_map/convert_element_type | solution.py:455
  265.8 0.0 copy-done
  265.9 0.0 copy-done.1
  265.9 0.0 copy-done.2
  265.9 6.2 %fusion.8 = (bf16[2,1024,512]{2,1,0:T(8,128)(2,1)}, f32[2,1024,512]{2,1,0:T(8,128)}, f32[2,1024,512]{2,1,0:T(8,128)}) fusion(bf16[2,1024,512]{2,1,0:T(8,128)(2,1)S(1)} %copy-done, f32[]{:T(128)S(6)} %min_shard_map.3, bf16[2,1024,512]{2,1,0:T(8,128)(2,1)S(1)} %copy-done.2, f32[2,1024,512]{2,1,0:T(8,128)S(1)} %copy-done.1, f32[2,1024,512]{2,1,0:T(8,128)} %param.18), kind=kLoop, calls=%fused_computation.17 | loop fusion | flops 17825792 | bytes 23068676 | tf_op jit(solution)/shard_map/convert_element_type | solution.py:455
Async XLA Ops:
  248.4 17.5 %copy-start = (bf16[2,1024,512]{2,1,0:T(8,128)(2,1)S(1)}, bf16[2,1024,512]{2,1,0:T(8,128)(2,1)}, u32[]{:S(2)}) copy-start(bf16[2,1024,512]{2,1,0:T(8,128)(2,1)} %wd_ref.1) | copy-start | bytes 6291460
  248.4 17.4 %copy-start.1 = (f32[2,1024,512]{2,1,0:T(8,128)S(1)}, f32[2,1024,512]{2,1,0:T(8,128)}, u32[]{:S(2)}) copy-start(f32[2,1024,512]{2,1,0:T(8,128)} %param.21) | copy-start | bytes 12582916
  248.4 17.4 %copy-start.2 = (bf16[2,1024,512]{2,1,0:T(8,128)(2,1)S(1)}, bf16[2,1024,512]{2,1,0:T(8,128)(2,1)}, u32[]{:S(2)}) copy-start(bf16[2,1024,512]{2,1,0:T(8,128)(2,1)} %get-tuple-element.16) | copy-start | bytes 6291460

commit v3 on v2

--- a/solution.py
+++ b/solution.py
@@ -161,9 +161,10 @@
     def forward(i, _):
         arrive(i)
         for t in range(T // TT):
+            if t != 1:
+                pump_x(3 * i + 5 + max(t - 1, 0))
             if t > 0:
-                pump_x(3 * i + t + 4)
-                pump_y(3 * i + t + 2)
+                pump_y(3 * i + 2 + t)
             rows = slice(t * TT, (t + 1) * TT)
             a = A0[rows, :]
             gate, up = dot(a, matrix(0, i, 0)), dot(a, matrix(0, i, 1))
@@ -296,7 +297,7 @@
         def _():
             final(q - 4)
 
-        @pl.when((q >= 1) & (q != CH) & (q != CH + 1))
+        @pl.when((q >= 1) & (q != CH))
         def _():
             on_chip(q - 1)
 
@@ -325,20 +326,16 @@
                     arrive(CH + i + 1)
 
             both(2 * j, 0, l)
-            both(2 * j + 1, 1, l)
 
             @pl.when(lax.rem(j, 2) == 0)
             def _():
                 sums(q0 + i)
 
+            both(2 * j + 1, 1, l)
+
             @pl.when(lax.rem(j, 2) == 1)
             def _():
                 emit(q0 + i)
-                if l == 0:
-
-                    @pl.when(i == 0)
-                    def _():
-                        on_chip(CH)
 
             return 0
 

time: 272 us -> 261 us (0.960)
  Pallas kernels: 246 us -> 235 us
    pallas_call x1, Pallas kernels: 246 us -> 235 us  [gradients(): pl.pallas_call(kernel, out_shape=(jax.ShapeDtypeStruct(wg.shape, BF16), j...]
where the time goes in v3:
time: 261 us
  Pallas kernels  235 us (90%)
  other arithmetic  24.9 us (10%)
    pallas_call x1, Pallas kernels, gradients(): pl.pallas_call(kernel, out_shape=(jax.ShapeDtypeStruct(wg.shape, BF16), j...  235 us
    convert_element_type x2, other arithmetic, adamw(): return ((w - 0.02 * step).astype(BF16), m, v)  23.6 us

profile of v3, /device:TPU:0, one launch (start us, length us, event | category | flops | bytes accessed | tf_op | source)
XLA Modules:
  0.0 261.0 jit_solution(16297205507406383681)
XLA Ops:
  0.6 234.7 %step.1 = (bf16[2,128,4096]{2,1,0:T(8,128)(2,1)}, bf16[2,128,4096]{2,1,0:T(8,128)(2,1)}, bf16[2,1024,512]{2,1,0:T(8,128)(2,1)}, f32[8,128]{1,0:T(8,128)}) custom-call(bf16[2048,512]{1,0:T(8,128)(2,1)} %bitcast.2, bf16[2048,512]{1,0:T(8,128)(2,1)} %bitcast.3, bf16[2,128,4096]{2,1,0:T(8,128)(2,1)} %wg_ref.1, bf16[2,128,4096]{2,1,0:T(8,128)(2,1)} %wu_ref.1, ...), custom_call_target="tpu_custom_call" | custom-call | tf_op jit(solution)/shard_map/step/pallas_call | solution.py:408
  235.3 1.3 reduce_sum.9
  237.3 0.0 copy-start
  237.3 0.0 copy-start.1
  237.3 0.0 copy-start.2
  237.3 17.4 %fusion.2 = (bf16[2,128,4096]{2,1,0:T(8,128)(2,1)}, f32[2,128,4096]{2,1,0:T(8,128)}, f32[2,128,4096]{2,1,0:T(8,128)}, bf16[2,128,4096]{2,1,0:T(8,128)(2,1)}, f32...) fusion(bf16[2,128,4096]{2,1,0:T(8,128)(2,1)} %wg_ref.1, f32[]{:T(128)S(6)} %min_shard_map.3, ...), kind=kLoop, calls=%fused_computation.11 | loop fusion | flops 35651584 | bytes 46137348 | tf_op jit(solution)/shard_map/convert_element_type | solution.py:452
  254.8 0.0 copy-done
  254.8 0.0 copy-done.1
  254.8 0.0 copy-done.2
  254.8 6.2 %fusion.8 = (bf16[2,1024,512]{2,1,0:T(8,128)(2,1)}, f32[2,1024,512]{2,1,0:T(8,128)}, f32[2,1024,512]{2,1,0:T(8,128)}) fusion(bf16[2,1024,512]{2,1,0:T(8,128)(2,1)S(1)} %copy-done, f32[]{:T(128)S(6)} %min_shard_map.3, bf16[2,1024,512]{2,1,0:T(8,128)(2,1)S(1)} %copy-done.2, f32[2,1024,512]{2,1,0:T(8,128)S(1)} %copy-done.1, f32[2,1024,512]{2,1,0:T(8,128)} %param.18), kind=kLoop, calls=%fused_computation.17 | loop fusion | flops 17825792 | bytes 23068676 | tf_op jit(solution)/shard_map/convert_element_type | solution.py:452
Async XLA Ops:
  237.3 17.5 %copy-start = (bf16[2,1024,512]{2,1,0:T(8,128)(2,1)S(1)}, bf16[2,1024,512]{2,1,0:T(8,128)(2,1)}, u32[]{:S(2)}) copy-start(bf16[2,1024,512]{2,1,0:T(8,128)(2,1)} %wd_ref.1) | copy-start | bytes 6291460
  237.3 17.4 %copy-start.1 = (f32[2,1024,512]{2,1,0:T(8,128)S(1)}, f32[2,1024,512]{2,1,0:T(8,128)}, u32[]{:S(2)}) copy-start(f32[2,1024,512]{2,1,0:T(8,128)} %param.21) | copy-start | bytes 12582916
  237.3 17.4 %copy-start.2 = (bf16[2,1024,512]{2,1,0:T(8,128)(2,1)S(1)}, bf16[2,1024,512]{2,1,0:T(8,128)(2,1)}, u32[]{:S(2)}) copy-start(bf16[2,1024,512]{2,1,0:T(8,128)(2,1)} %get-tuple-element.16) | copy-start | bytes 6291460
